TPU v7x, 256 devices: a whole 4x4x8 slice. The times are simulated.
256 devices in a mesh: wide: 64 (over x, y_hi, z), narrow: 4 (over y_lo, core).
Axes of the slice: x: 4, y: 4 (y_hi: 2, y_lo: 2; y = y_hi * 2 + y_lo), z: 8, core: 2. Of those that a mesh axis runs over, the one named last changes fastest.
Arguments:
- tokens: bfloat16 [8192, 2048], P('wide'), may hold values from -6 to 6
- expert_ids: int32 [8192, 6], P('wide'), may hold values from 0 to 63, all different within a row; in each aligned block of 128 rows (0 to 127, 128 to 255, ...) at most 16 rows name the same one
- gate_weights: float32 [8192, 6], P('wide'), may hold values from 0.05 to 0.6
- shared_gate: bfloat16 [2048, 2816], P('wide', 'narrow'), may hold values from -0.125 to 0.125
- shared_up: bfloat16 [2048, 2816], P('wide', 'narrow'), may hold values from -0.125 to 0.125
- shared_down: bfloat16 [2816, 2048], P('narrow', 'wide'), may hold values from -0.109375 to 0.109375
- expert_gate: bfloat16 [64, 2048, 1408], P('wide', None, 'narrow'), may hold values from -0.125 to 0.125
- expert_up: bfloat16 [64, 2048, 1408], P('wide', None, 'narrow'), may hold values from -0.125 to 0.125
- expert_down: bfloat16 [64, 1408, 2048], P('wide', 'narrow'), may hold values from -0.15625 to 0.15625
Outputs:
- moe_out: bfloat16 [8192, 2048], P('wide', 'narrow')
Inputs may be any that keep to these rules, and one draw needn't show every extreme that they name: `expert_ids`: the 6 ids of a row differ. Among the 128 rows of one index of wide, no expert is named by more than 16 rows.
All inputs are finite; a program needn't handle non-finite values.
Results may differ from a plain program's by a relative error of at most 0.0075.
Values may be sent and summed in bfloat16 or wider, within the bound.
A program may use at most 128 MiB of HBM per device.

v0:
```python
import jax
import jax.numpy as jnp
from jax import lax
from jax.sharding import PartitionSpec as P


def items_in_groups(array, axis, split_dim, concat_dim, work, item_dim, out_dim):
    items = jax.tree.leaves(array)[0].shape[item_dim]
    count = 2 if items % 2 == 0 else 1
    finished = []
    for k in range(count):
        group = jax.tree.map(
            lambda a: lax.slice_in_dim(
                a, k * (items // count), (k + 1) * (items // count), axis=item_dim
            ),
            array,
        )
        finished.append(
            work(
                lax.all_to_all(
                    group, axis, split_axis=split_dim, concat_axis=concat_dim, tiled=True
                )
            )
        )
    return jax.tree.map(lambda *parts: jnp.concatenate(parts, axis=out_dim), *finished)


def split_up(array, dim, length):
    lengths = array.shape
    blocks = array.reshape(*lengths[:dim], length, lengths[dim] // length, *lengths[dim + 1 :])
    return jnp.moveaxis(blocks, dim, 0)


def sum_at_owner(array, axis, dim):
    length = lax.axis_size(axis)
    blocks = lax.all_to_all(split_up(array, dim, length), axis, 0, 0, tiled=True)
    return jnp.sum(blocks.astype(jnp.float32), axis=0)


def sent_together(arrays, axis, dim, along):
    ends, at = ([], 0)
    for a in arrays[:-1]:
        at += a.shape[along]
        ends.append(at)
    both = jnp.concatenate(arrays, axis=along)
    return tuple(jnp.split(lax.all_gather(both, axis, axis=dim, tiled=True), ends, axis=along))


def expert_ffn(received, w_gate, w_up, w_down):
    senders, items, width = received.shape
    flat_rows = received.reshape(senders * items, width)
    gate_part = jnp.dot(flat_rows, w_gate, preferred_element_type=jnp.float32)
    up_part = jnp.dot(flat_rows, w_up, preferred_element_type=jnp.float32)
    hidden = (jax.nn.silu(gate_part) * up_part).astype(jnp.bfloat16)
    partial_value = jnp.dot(hidden, w_down, preferred_element_type=jnp.float32).astype(jnp.bfloat16)
    return partial_value.reshape(senders, items, w_down.shape[1])


def body(
    tokens,
    expert_ids,
    gate_weights,
    shared_gate,
    shared_up,
    shared_down,
    expert_gate,
    expert_up,
    expert_down,
):
    tok_count, width = tokens.shape
    top_count = expert_ids.shape[1]
    experts = lax.axis_size("wide") * expert_gate.shape[0]
    capacity = min(tok_count, 4 * tok_count * top_count // (3 * experts))
    w_gate = expert_gate[0]
    w_up = expert_up[0]
    w_down = expert_down[0]
    pairs = tok_count * top_count
    flat_ids = expert_ids.reshape(pairs)
    onehot = (flat_ids[:, None] == jnp.arange(experts, dtype=jnp.int32)[None, :]).astype(jnp.int32)
    before = jnp.cumsum(onehot, axis=0) - onehot
    slot_pos = jnp.sum(before * onehot, axis=1)
    target_slot = flat_ids * capacity + slot_pos
    source = (
        jnp.full((experts * capacity,), -1, jnp.int32)
        .at[target_slot]
        .set(jnp.arange(pairs, dtype=jnp.int32))
    )
    filled = source >= 0
    token_of = jnp.where(filled, source // top_count, 0)
    outgoing = jnp.where(filled[:, None], tokens[token_of], jnp.zeros((), jnp.bfloat16))
    outgoing = outgoing.reshape(experts, capacity, width)

    def run_expert(received):
        return expert_ffn(received, w_gate, w_up, w_down)

    partial_value = items_in_groups(outgoing, "wide", 0, 0, run_expert, 1, 1)
    expert_out = sum_at_owner(partial_value, "narrow", 2).astype(jnp.bfloat16)
    returned = lax.all_to_all(expert_out, "wide", split_axis=0, concat_axis=0, tiled=True)
    returned_rows = returned.reshape(experts * capacity, returned.shape[2])
    pair_rows = returned_rows[target_slot].astype(jnp.float32)
    weighted = gate_weights.reshape(pairs, 1) * pair_rows
    routed = jnp.sum(weighted.reshape(tok_count, top_count, returned.shape[2]), axis=1)
    blocks = sent_together((shared_gate, shared_up), "wide", 0, 1)
    gate_sum = jnp.dot(tokens, blocks[0], preferred_element_type=jnp.float32)
    up_sum = jnp.dot(tokens, blocks[1], preferred_element_type=jnp.float32)
    shared_hidden = (jax.nn.silu(gate_sum) * up_sum).astype(jnp.bfloat16)
    shared_terms = jnp.dot(
        shared_hidden,
        lax.all_gather(shared_down, "wide", axis=1, tiled=True),
        preferred_element_type=jnp.float32,
    )
    shared = sum_at_owner(shared_terms.astype(jnp.bfloat16), "narrow", 1)
    return (shared + routed).astype(jnp.bfloat16)


def solution(mesh):
    in_specs = (
        P("wide", None),
        P("wide", None),
        P("wide", None),
        P("wide", "narrow"),
        P("wide", "narrow"),
        P("narrow", "wide"),
        P("wide", None, "narrow"),
        P("wide", None, "narrow"),
        P("wide", "narrow", None),
    )
    out_specs = P("wide", "narrow")
    return jax.shard_map(body, mesh=mesh, in_specs=in_specs, out_specs=out_specs, check_vma=False)
```

profile of v0, /device:TPU:1, one launch (start us, length us, event | category | flops | bytes accessed | tf_op | source)
XLA Modules:
  0.0 334.1 jit_solution(4834467579335310039)
XLA Ops:
  6.5 1.7 pad_maximum_fusion.1
  10.3 1.8 reduce-window.6
  12.6 3.4 %scatter_custom_fusion = s32[1024]{0:T(1024)S(1)} fusion(s32[768]{0:T(1024)S(1)} %fusion.85, s32[768]{0:T(1024)S(1)} %iota.11, s32[]{:T(128)} %constant.16.clone.1), kind=kCustom, calls=%fused_computation.79 | custom fusion | bytes 4100 | tf_op jit(solution)/shard_map/scatter | solution.py:86
  16.1 6.1 %gather_fusion = bf16[1024,2048]{1,0:T(8,128)(2,1)} fusion(bf16[128,2048]{1,0:T(8,128)(2,1)S(1)} %copy-done.1, s32[1024]{0:T(1024)S(1)} %fusion.83), kind=kCustom, calls=%fused_computation | custom fusion | bytes 8392704 | tf_op jit(solution)/shard_map/gather | solution.py:90
  22.2 2.5 broadcast_select_fusion
  24.7 1.8 fusion.91
  26.5 68.2 %all_to_all.25 = bf16[64,8,2048]{2,1,0:T(8,128)(2,1)} all-to-all(bf16[64,8,2048]{2,1,0:T(8,128)(2,1)S(1)} %get-tuple-element.6), channel_id=1, replica_groups=mesh['wide'=64,'narrow'=4] {'wide'}, dimensions={0} | all-to-all | bytes 4194304 | tf_op jit(solution)/shard_map/all_to_all | solution.py:20
  94.7 10.2 %all-to-all-start.1 = ((bf16[64,8,2048]{2,1,0:T(8,128)(2,1)}), bf16[64,8,2048]{2,1,0:T(8,128)(2,1)}, u32[]{:S(2)}, u32[]{:S(2)}) async-start(bf16[64,8,2048]{2,1,0:T(8,128)(2,1)} %get-tuple-element.5), calls=%async_computation.1 | async-start | bytes 4194304 | tf_op jit(solution)/shard_map/all_to_all | solution.py:20
  105.7 3.4 %fusion.6 = f32[512,352]{0,1:T(8,128)} fusion(bf16[64,8,2048]{2,1,0:T(8,128)(2,1)} %all_to_all.25, bf16[1,2048,352]{1,2,0:T(8,128)(2,1)S(1)} %copy-done.3), kind=kOutput, calls=%fused_computation.15 | convolution fusion | flops 738197504 | bytes 4259840 | tf_op jit(solution)/shard_map/dot_general | solution.py:52
  109.1 5.7 %convolution_convert_fusion = bf16[512,2048]{1,0:T(8,128)(2,1)} fusion(bf16[1,352,2048]{2,1,0:T(8,128)(2,1)S(1)} %copy-done, bf16[1,2048,352]{1,2,0:T(8,128)(2,1)} %param.16, bf16[64,8,2048]{2,1,0:T(8,128)(2,1)} %all_to_all.25, f32[512,352]{0,1:T(8,128)} %fusion.6), kind=kOutput, calls=%fused_computation.10 | convolution fusion | flops 1478524928 | bytes 7798784 | tf_op jit(solution)/shard_map/dot_general | solution.py:55
  114.8 46.5 %all-to-all-done.1 = bf16[64,8,2048]{2,1,0:T(8,128)(2,1)} async-done(((bf16[64,8,2048]{2,1,0:T(8,128)(2,1)}), bf16[64,8,2048]{2,1,0:T(8,128)(2,1)}, u32[]{:S(2)}, u32[]{:S(2)}) %all-to-all-start.1) | async-done | bytes 2097184 | tf_op jit(solution)/shard_map/all_to_all | solution.py:20
  161.3 3.4 %fusion.10 = f32[512,352]{0,1:T(8,128)} fusion(bf16[64,8,2048]{2,1,0:T(8,128)(2,1)} %all-to-all-done.1, bf16[1,2048,352]{1,2,0:T(8,128)(2,1)S(1)} %copy-done.3), kind=kOutput, calls=%fused_computation.19 | convolution fusion | flops 738197504 | bytes 4259840 | tf_op jit(solution)/shard_map/dot_general | solution.py:52
  164.7 5.8 %convolution_convert_fusion.1 = bf16[512,2048]{1,0:T(8,128)(2,1)} fusion(bf16[1,352,2048]{2,1,0:T(8,128)(2,1)S(1)} %copy-done, bf16[1,2048,352]{1,2,0:T(8,128)(2,1)} %param.16, bf16[64,8,2048]{2,1,0:T(8,128)(2,1)} %all-to-all-done.1, f32[512,352]{0,1:T(8,128)} %fusion.10), kind=kOutput, calls=%fused_computation.11 | convolution fusion | flops 1478524928 | bytes 7798784 | tf_op jit(solution)/shard_map/dot_general | solution.py:55
  170.5 2.5 copy_bitcast_fusion
  173.0 59.4 %all_to_all.26 = bf16[4,64,16,512]{3,2,1,0:T(8,128)(2,1)} all-to-all(bf16[4,64,16,512]{3,2,1,0:T(8,128)(2,1)S(1)} %copy_bitcast_fusion), channel_id=1, replica_groups=mesh['wide'=64,'narrow'=4] {'narrow'}, dimensions={0} | all-to-all | bytes 8388608 | tf_op jit(solution)/shard_map/all_to_all | solution.py:36
  232.4 4.4 %reduce_sum.44 = bf16[64,16,512]{2,1,0:T(8,128)(2,1)} reduce(bf16[4,64,16,512]{3,2,1,0:T(8,128)(2,1)} %all_to_all.26, bf16[]{:T(256)} %constant.35.clone.1), dimensions={0}, to_apply=%region_5.6 | reduce | flops 1572864 | bytes 5242882 | tf_op jit(solution)/shard_map/reduce_sum | solution.py:37
  236.9 9.4 %all-to-all-start.4 = ((bf16[64,16,512]{2,1,0:T(8,128)(2,1)}), bf16[64,16,512]{2,1,0:T(8,128)(2,1)S(1)}, u32[]{:S(2)}, u32[]{:S(2)}) async-start(bf16[64,16,512]{2,1,0:T(8,128)(2,1)} %reduce_sum.44), calls=%async_computation.4 | async-start | bytes 2097152 | tf_op jit(solution)/shard_map/all_to_all | solution.py:98
  246.3 3.6 %fusion.38 = f32[128,704]{0,1:T(8,128)} fusion(bf16[128,2048]{1,0:T(8,128)(2,1)S(1)} %copy-done.1, bf16[2048,1408]{1,0:T(8,128)(2,1)} %all-gather.3.cloned.1.call-done), kind=kOutput, calls=%fused_computation.32 | convolution fusion | flops 369098752 | bytes 4030464 | tf_op jit(solution)/shard_map/dot_general | solution.py:104
  250.0 50.0 %all-gather.5.cloned.1.call-done = bf16[704,2048]{0,1:T(8,128)(2,1)} async-done(((bf16[704,32]{0,1:T(8,128)(2,1)}), bf16[704,2048]{0,1:T(8,128)(2,1)}) %all-gather.5.cloned.1.call-update) | async-done | bytes 2883600 | tf_op jit(solution)/shard_map/all_gather | solution.py:109
  299.9 7.4 %convolution_convert_fusion.2 = bf16[128,2048]{1,0:T(8,128)(2,1)S(1)} fusion(bf16[704,2048]{0,1:T(8,128)(2,1)} %all-gather.5.cloned.1.call-done, bf16[128,2048]{1,0:T(8,128)(2,1)S(1)} %copy-done.1, bf16[2048,1408]{1,0:T(8,128)(2,1)} %all-gather.3.cloned.1.call-done, f32[128,704]{0,1:T(8,128)} %fusion.38), kind=kOutput, calls=%fused_computation.12 | convolution fusion | flops 739000320 | bytes 7700480 | tf_op jit(solution)/shard_map/dot_general | solution.py:107
  308.2 8.4 %all-to-all-start = ((bf16[4,128,512]{2,1,0:T(8,128)(2,1)}), bf16[4,128,512]{2,1,0:T(8,128)(2,1)}, u32[]{:S(2)}, u32[]{:S(2)}) async-start(bf16[4,128,512]{2,1,0:T(8,128)(2,1)} %bitcast.93), calls=%async_computation | async-start | bytes 1048576 | tf_op jit(solution)/shard_map/all_to_all | solution.py:36
  317.3 3.3 gather_fusion.1
  321.9 2.2 multiply_reduce_fusion
  325.7 1.6 add_convert_fusion
  (35 shorter events, 7.8 us)
Async XLA Ops:
  6.5 102.6 %copy-start = (bf16[1,352,2048]{2,1,0:T(8,128)(2,1)S(1)}, bf16[1,352,2048]{2,1,0:T(8,128)(2,1)}, u32[]{:S(2)}) copy-start(bf16[1,352,2048]{2,1,0:T(8,128)(2,1)} %param.17) | copy-start | bytes 4325380
  6.5 9.6 %copy-start.1 = (bf16[128,2048]{1,0:T(8,128)(2,1)S(1)}, bf16[128,2048]{1,0:T(8,128)(2,1)}, u32[]{:S(2)}) copy-start(bf16[128,2048]{1,0:T(8,128)(2,1)} %param.9) | copy-start | bytes 1572868
  6.5 239.8 %all-gather.3.cloned.1.call-start = ((), (), s32[]{:S(2)}) async-start(), calls=%async_computation.5 | async-start | bytes 5857280 | tf_op jit(solution)/shard_map/all_gather | solution.py:46
  94.7 11.0 %copy-start.3 = (bf16[1,2048,352]{1,2,0:T(8,128)(2,1)S(1)}, bf16[1,2048,352]{1,2,0:T(8,128)(2,1)}, u32[]{:S(2)}) copy-start(bf16[1,2048,352]{1,2,0:T(8,128)(2,1)} %param.15) | copy-start | bytes 4325380
  94.7 66.6 %all-to-all-start.1 = ((bf16[64,8,2048]{2,1,0:T(8,128)(2,1)}), bf16[64,8,2048]{2,1,0:T(8,128)(2,1)}, u32[]{:S(2)}, u32[]{:S(2)}) async-start(bf16[64,8,2048]{2,1,0:T(8,128)(2,1)} %get-tuple-element.5), calls=%async_computation.1 | async-start | bytes 4194304 | tf_op jit(solution)/shard_map/all_to_all | solution.py:20
  104.9 195.0 %all-gather.5.cloned.1.call-start = ((), (), s32[]{:S(2)}) async-start(), calls=%async_computation.6 | async-start | bytes 3194880 | tf_op jit(solution)/shard_map/all_gather | solution.py:109
  236.9 71.3 %all-to-all-start.4 = ((bf16[64,16,512]{2,1,0:T(8,128)(2,1)}), bf16[64,16,512]{2,1,0:T(8,128)(2,1)S(1)}, u32[]{:S(2)}, u32[]{:S(2)}) async-start(bf16[64,16,512]{2,1,0:T(8,128)(2,1)} %reduce_sum.44), calls=%async_computation.4 | async-start | bytes 2097152 | tf_op jit(solution)/shard_map/all_to_all | solution.py:98
  307.3 9.2 %copy-start.2 = (f32[128,6]{0,1:T(8,128)S(1)}, f32[128,6]{0,1:T(8,128)}, u32[]{:S(2)}) copy-start(f32[128,6]{0,1:T(8,128)} %param.11) | copy-start | bytes 9220
  308.2 16.3 %all-to-all-start = ((bf16[4,128,512]{2,1,0:T(8,128)(2,1)}), bf16[4,128,512]{2,1,0:T(8,128)(2,1)}, u32[]{:S(2)}, u32[]{:S(2)}) async-start(bf16[4,128,512]{2,1,0:T(8,128)(2,1)} %bitcast.93), calls=%async_computation | async-start | bytes 1048576 | tf_op jit(solution)/shard_map/all_to_all | solution.py:36
Sparse Core Ops, SparseCore 0:
  10.8 162.8 all-gather.2
  177.4 122.4 all-gather.4
where the time goes:
time: 335 us; the launch traced here: 334 us
  blocking collectives  128 us (38%)
  waiting for transfers between devices  97.5 us (29%)
  matrix products  29.3 us (9%)
  starting transfers between devices  28.1 us (8%)
  local copies, waits for them, and re-layouts  19.1 us (6%)
  other arithmetic  18.9 us (6%)
  between operations  13.6 us (4%)
    all_to_all x1, blocking collectives, items_in_groups(): lax.all_to_all(group, axis, split_axis=split_dim, concat_axis=concat_dim,...  68.2 us
    all_to_all x1, blocking collectives, sum_at_owner(): lax.all_to_all(split_up(array, dim, length), axis, 0, 0, tiled=True)  59.4 us
    all_gather x1, waiting for transfers between devices, body(): lax.all_gather(shared_down, 'wide', axis=1, tiled=True)  50 us
    all_to_all x1, waiting for transfers between devices, items_in_groups(): lax.all_to_all(group, axis, split_axis=split_dim, concat_axis=concat_dim,...  46.5 us
    dot_general x2, matrix products, expert_ffn(): jnp.dot(hidden, w_down, preferred_element_type=jnp.float32)  11.5 us
    all_to_all x1, starting transfers between devices, items_in_groups(): lax.all_to_all(group, axis, split_axis=split_dim, concat_axis=concat_dim,...  10.2 us
    all_to_all x1, starting transfers between devices, body(): lax.all_to_all(expert_out, 'wide', split_axis=0, concat_axis=0, tiled=True)  9.44 us
    all_to_all x1, starting transfers between devices, sum_at_owner(): lax.all_to_all(split_up(array, dim, length), axis, 0, 0, tiled=True)  8.38 us
  transfers between devices with their start and end apart: 5, of which 3 were waited for; matrix products, arithmetic and copies ran while one was open for 19% of the time, Pallas kernels for 0%

commit v1 on v0

v1 whole, which is shorter than its diff:
```python
import jax
import jax.numpy as jnp
from jax import lax
from jax.experimental import pallas as pl
from jax.experimental.pallas import tpu as pltpu
from jax.sharding import PartitionSpec as P

MESH = pl.DeviceIdType.MESH
BF16 = jnp.bfloat16
F32 = jnp.float32

NX, NY, NZ = 4, 2, 8
CAP = 16
GROUPS = NX * NY
ROWS = NZ * CAP
TOK = 128
D = 2048
Q = D // 4
H = 352
UNIT_ORDER = (0, 7, 1, 6, 2, 5, 3, 4)


def silu_mul(g, u):
    return (g * jax.nn.sigmoid(g) * u).astype(BF16)


def dot(a, b):
    return jnp.dot(a, b, preferred_element_type=F32)


def dot_t(a, b):
    return lax.dot_general(a, b, (((1,), (1,)), ((), ())), preferred_element_type=F32)


def kernel(
    tok, ids, gws, wp, eg, eu, ed, out,
    outg, full, wg, wu, wd, pbuf, r1, sbuf, keep, r2, fin, ret, whi, wlo, rank, gate, wall,
    ds_s, ds_r, a1_s, a1_r, a2_s, a2_r, b_s, b_r, r1_s, r1_r, r2_s, r2_r, rt_s, rt_r,
    w0_s, w0_r, zc_s, zc_r, zd_s, zd_r, xp_s, xp_r, xm_s, xm_r, xf_s, xf_r, xg_s, xg_r, l_s,
):
    w = lax.axis_index("wide")
    n = lax.axis_index("narrow")
    x, yh, z = w // (NY * NZ), (w // NZ) % NY, w % NZ
    a, c = n // 2, n % 2

    def dev(xx, yy, zz):
        return ((xx % NX) * NY + yy % NY) * NZ + zz % NZ

    mate = (w, 2 * a + 1 - c)
    over = (w, 2 * (1 - a) + c)
    n_mate, n_over, n_diag = mate[1], over[1], 2 * (1 - a) + 1 - c

    def remote(src, dst, ssem, rsem, device):
        return pltpu.make_async_remote_copy(
            src_ref=src, dst_ref=dst, send_sem=ssem, recv_sem=rsem,
            device_id=device, device_id_type=MESH,
        )

    def wait(ref, sem):
        pltpu.make_async_copy(ref, ref, sem).wait()

    barrier = pltpu.get_barrier_semaphore()

    def greet(d, carry):
        dx, dy, dz = d // (NY * NZ), (d // NZ) % NY, d % NZ
        pl.semaphore_signal(
            barrier, inc=1, device_id=(dev(x + dx, yh + dy, z + dz), n), device_id_type=MESH
        )
        return carry

    lax.fori_loop(1, NX * NY * NZ, greet, 0)
    pl.semaphore_signal(barrier, inc=1, device_id=mate, device_id_type=MESH)
    pl.semaphore_signal(barrier, inc=1, device_id=over, device_id_type=MESH)

    loads = (
        pltpu.make_async_copy(eg.at[0], wg, l_s.at[0]),
        pltpu.make_async_copy(eu.at[0], wu, l_s.at[1]),
        pltpu.make_async_copy(ed.at[0], wd, l_s.at[2]),
    )
    for load in loads:
        load.start()

    expert = lax.broadcasted_iota(jnp.int32, (NX * NY * NZ, TOK), 0)
    named = jnp.zeros((NX * NY * NZ, TOK), F32)
    weight = jnp.zeros((NX * NY * NZ, TOK), F32)
    for k in range(6):
        hit = ids[k : k + 1, :] == expert
        named = jnp.where(hit, 1.0, named)
        weight = jnp.where(hit, gws[k : k + 1, :], weight)
    upper = (
        lax.broadcasted_iota(jnp.int32, (TOK, TOK), 0)
        < lax.broadcasted_iota(jnp.int32, (TOK, TOK), 1)
    )
    before = dot(named.astype(BF16), jnp.where(upper, 1.0, 0.0).astype(BF16))
    rank[...] = jnp.where(named > 0.0, before, -1.0)
    gate[...] = weight
    wall[x, z, yh] = wp[yh]

    pl.semaphore_wait(barrier, NX * NY * NZ - 1 + 2)

    partner = (dev(x, yh + 1, z), n)
    w0 = remote(wp.at[1 - yh], wall.at[x, z, yh], w0_s, w0_r, partner)
    w0.start()
    to_partner = remote(
        tok.at[:, pl.ds(pl.multiple_of(n * Q, Q), Q)], full.at[GROUPS, n],
        ds_s.at[GROUPS, 0], ds_r.at[GROUPS, 0], partner,
    )

    slot = (lax.broadcasted_iota(jnp.int32, (ROWS, TOK), 0) % CAP).astype(F32)
    owner = lax.broadcasted_iota(jnp.int32, (ROWS, NZ), 0) // CAP
    spread = jnp.where(
        owner == lax.broadcasted_iota(jnp.int32, (ROWS, NZ), 1), 1.0, 0.0
    ).astype(BF16)

    def group_rank(g):
        e0 = pl.multiple_of(dev(x + g // NY, yh + g % NY, 0), NZ)
        return e0, dot(spread, rank[pl.ds(e0, NZ), :].astype(BF16)) == slot

    def send_copy(g, dz):
        zt = (z + dz) % NZ
        return remote(
            outg.at[g, pl.ds(zt * CAP, CAP)], full.at[g, n, pl.ds(z * CAP, CAP)],
            ds_s.at[g, dz], ds_r.at[g, dz], (dev(x + g // NY, yh + g % NY, zt), n),
        )

    def dispatch(g, carry):
        e0, hit = group_rank(g)
        pick = jnp.where(hit, 1.0, 0.0).astype(BF16)
        outg[g] = dot(pick, tok[:, pl.ds(pl.multiple_of(n * Q, Q), Q)]).astype(BF16)
        for dz in range(1, NZ):
            send_copy(g, dz).start()

        @pl.when(g > 0)
        def _():
            send_copy(g, 0).start()

        return carry

    lax.fori_loop(0, GROUPS, dispatch, 0)
    mine = pl.ds(z * CAP, CAP)
    full[0, n, mine] = outg[0, mine]
    to_partner.start()

    def weights(g, carry):
        e0, hit = group_rank(g)
        gw = gate[pl.ds(e0, NZ), :]
        gw_hi = gw.astype(BF16)
        gw_lo = (gw - gw_hi.astype(F32)).astype(BF16)
        zero = jnp.zeros((ROWS, TOK), F32)
        whi[g] = jnp.where(hit, dot(spread, gw_hi), zero).T.astype(BF16)
        wlo[g] = jnp.where(hit, dot(spread, gw_lo), zero).T.astype(BF16)
        return carry

    lax.fori_loop(0, GROUPS, weights, 0)

    def unit(xx, dz):
        return wall.at[xx % NX, (z + dz) % NZ]

    def x_send(dz):
        u = unit(x, dz)
        return (
            remote(u, u, xp_s.at[dz], xp_r.at[dz], (dev(x + 1, yh, z), n)),
            remote(u, u, xm_s.at[dz], xm_r.at[dz], (dev(x + NX - 1, yh, z), n)),
        )

    def x_forward(dz):
        lower = unit(x + NX - 1, dz).at[0]
        upper = unit(x + 1, dz).at[1]
        return (
            remote(lower, lower, xf_s.at[dz], xf_r.at[dz], (dev(x + 1, yh, z), n)),
            remote(upper, upper, xg_s.at[dz], xg_r.at[dz], (dev(x + NX - 1, yh, z), n)),
        )

    def z_send(s):
        up, down = unit(x, NZ - s), unit(x, s)
        if s == 3:
            up, down = up.at[0], down.at[1]
        return (
            remote(up, up, zc_s.at[s], zc_r.at[s], (dev(x, yh, z + 1), n)),
            remote(down, down, zd_s.at[s], zd_r.at[s], (dev(x, yh, z + NZ - 1), n)),
        )

    def ring(s):
        if s == 0:
            wait(wall.at[x, z, 1 - yh], w0_r)
        elif s < 4:
            wait(unit(x, NZ - s), zc_r.at[s - 1])
            wait(unit(x, s), zd_r.at[s - 1])
        else:
            wait(unit(x, 4).at[0], zc_r.at[3])
            wait(unit(x, 4).at[1], zd_r.at[3])
        if s < 4:
            for copy in z_send(s):
                copy.start()
        for dz in sorted({s, (NZ - s) % NZ}):
            for copy in x_send(dz):
                copy.start()

    def forward(dz):
        wait(unit(x + NX - 1, dz), xp_r.at[dz])
        wait(unit(x + 1, dz), xm_r.at[dz])
        for copy in x_forward(dz):
            copy.start()

    ring(0)
    for load in loads:
        load.wait()

    def gather_mate(i):
        return remote(full.at[i, n], full.at[i, n], a1_s.at[i], a1_r.at[i], mate)

    def gather_over(i):
        return remote(full.at[i, n], full.at[i, n], a2_s.at[i], a2_r.at[i], over)

    def gather_diag(i):
        return remote(full.at[i, n_over], full.at[i, n_over], b_s.at[i], b_r.at[i], mate)

    def scatter_mate(i):
        return remote(pbuf.at[i, 1 - c], r1.at[i], r1_s.at[i], r1_r.at[i], mate)

    def scatter_over(i):
        return remote(sbuf.at[i], r2.at[i], r2_s.at[i], r2_r.at[i], over)

    def return_copy(g, dz):
        zs = (z + NZ - dz) % NZ
        return remote(
            fin.at[g, pl.ds(zs * CAP, CAP)], ret.at[g, pl.ds(z * CAP, CAP)],
            rt_s.at[g, dz], rt_r.at[g, dz],
            (dev(x + NX - g // NY, yh + NY - g % NY, zs), n),
        )

    to_home = remote(fin.at[GROUPS], ret.at[GROUPS], rt_s.at[GROUPS, 0], rt_r.at[GROUPS, 0], partner)

    def arrive(i):
        @pl.when(i < GROUPS)
        def _():
            for dz in range(1, NZ):
                wait(full.at[i, n, pl.ds(((z + NZ - dz) % NZ) * CAP, CAP)], ds_r.at[i, dz])

            @pl.when(i > 0)
            def _():
                wait(full.at[i, n, mine], ds_r.at[i, 0])

        @pl.when(i == GROUPS)
        def _():
            wait(full.at[GROUPS, n], ds_r.at[GROUPS, 0])

        gather_over(i).start()
        gather_mate(i).start()

    def pass_on(i):
        wait(full.at[i, n_over], a2_r.at[i])
        gather_diag(i).start()

    def gathered(i):
        wait(full.at[i, n_mate], a1_r.at[i])
        wait(full.at[i, n_diag], b_r.at[i])

    def ffn(i):
        gathered(i)
        gp = jnp.zeros((ROWS, H), F32)
        up = jnp.zeros((ROWS, H), F32)
        for q in range(4):
            rows = full[i, q]
            gp += dot(rows, wg[q * Q : (q + 1) * Q, :])
            up += dot(rows, wu[q * Q : (q + 1) * Q, :])
        hidden = silu_mul(gp, up)
        for q in range(4):
            pbuf[i, q % 2, q // 2] = dot(hidden, wd[:, q * Q : (q + 1) * Q]).astype(BF16)
        scatter_mate(i).start()

    def add_mate(i):
        wait(r1.at[i], r1_r.at[i])
        sbuf[i] = (pbuf[i, c, 1 - a].astype(F32) + r1[i, 1 - a].astype(F32)).astype(BF16)
        scatter_over(i).start()
        keep[i] = pbuf[i, c, a].astype(F32) + r1[i, a].astype(F32)

    def add_over(i):
        wait(r2.at[i], r2_r.at[i])
        return keep[i] + r2[i].astype(F32)

    def send_home(i):
        fin[i] = add_over(i).astype(BF16)
        for dz in range(1, NZ):
            return_copy(i, dz).start()

        @pl.when(i > 0)
        def _():
            return_copy(i, 0).start()

        @pl.when(i == 0)
        def _():
            ret[0, mine] = fin[0, mine]

    side = {1: [lambda: ring(1)], 3: [lambda: ring(2)], 5: [lambda: ring(3)], 7: [lambda: ring(4)]}
    for it, dzs in {2: (0,), 4: (7, 1), 6: (6, 2), 8: (5, 3), 10: (4,)}.items():
        side.setdefault(it, []).extend([lambda dz=dz: forward(dz) for dz in dzs])

    def step(i, carry):
        @pl.when(i <= GROUPS)
        def _():
            arrive(i)

        @pl.when((i >= 1) & (i <= GROUPS + 1))
        def _():
            pass_on(i - 1)

        @pl.when((i >= 2) & (i < GROUPS + 2))
        def _():
            ffn(i - 2)

        @pl.when((i >= 3) & (i < GROUPS + 3))
        def _():
            add_mate(i - 3)

        @pl.when((i >= 4) & (i < GROUPS + 4))
        def _():
            send_home(i - 4)

        for it, jobs in side.items():
            @pl.when(i == it)
            def _():
                for job in jobs:
                    job()

        return carry

    lax.fori_loop(0, GROUPS + 4, step, 0)

    for dz in range(NZ):
        wait(unit(x + 2, dz).at[0], xf_r.at[dz])
        wait(unit(x + 2, dz).at[1], xg_r.at[dz])
    gathered(GROUPS)
    gp = jnp.zeros((2 * TOK, H), F32)
    up = jnp.zeros((2 * TOK, H), F32)
    wide_block = NZ * 32
    for k in range(NX * NY):
        xx, yy = k // NY, k % NY
        rows = jnp.concatenate(
            [
                full[GROUPS, xx, :, yy * wide_block : (yy + 1) * wide_block],
                tok[:, k * wide_block : (k + 1) * wide_block],
            ],
            axis=0,
        )
        gp += dot(rows, wall[xx, :, yy, 0].reshape(wide_block, H))
        up += dot(rows, wall[xx, :, yy, 1].reshape(wide_block, H))
    hidden = silu_mul(gp, up)
    for k in range(NX * NY):
        xx, yy = k // NY, k % NY
        part = dot_t(hidden, wall[xx, :, yy, 2].reshape(wide_block, H)).astype(BF16)
        cols = slice(yy * wide_block, (yy + 1) * wide_block)
        pbuf[GROUPS, xx % 2, xx // 2, :, cols] = part[:TOK]
        pbuf[GROUPS + 1, xx % 2, xx // 2, :, cols] = part[TOK:]
    scatter_mate(GROUPS).start()
    scatter_mate(GROUPS + 1).start()

    def combine(lo, hi, acc):
        for g in range(lo, hi):
            for dz in range(1 if g == 0 else 0, NZ):
                wait(ret.at[g, pl.ds(((z + dz) % NZ) * CAP, CAP)], rt_r.at[g, dz])
            acc = acc + dot(whi[g], ret[g]) + dot(wlo[g], ret[g])
        return acc

    acc = combine(0, GROUPS // 2, jnp.zeros((TOK, Q), F32))
    add_mate(GROUPS)
    add_mate(GROUPS + 1)
    acc = combine(GROUPS // 2, GROUPS, acc)
    fin[GROUPS] = add_over(GROUPS).astype(BF16)
    to_home.start()
    acc = acc + add_over(GROUPS + 1)
    wait(ret.at[GROUPS], rt_r.at[GROUPS, 0])
    out[...] = (acc + ret[GROUPS].astype(F32)).astype(BF16)

    w0.wait_send()
    to_partner.wait_send()
    to_home.wait_send()

    def drain(g, carry):
        for dz in range(1, NZ):
            send_copy(g, dz).wait_send()
            return_copy(g, dz).wait_send()

        @pl.when(g > 0)
        def _():
            send_copy(g, 0).wait_send()
            return_copy(g, 0).wait_send()

        return carry

    lax.fori_loop(0, GROUPS, drain, 0)

    def drain_narrow(i, carry):
        gather_over(i).wait_send()
        gather_mate(i).wait_send()
        gather_diag(i).wait_send()
        scatter_mate(i).wait_send()
        scatter_over(i).wait_send()
        return carry

    lax.fori_loop(0, GROUPS + 1, drain_narrow, 0)
    scatter_mate(GROUPS + 1).wait_send()
    scatter_over(GROUPS + 1).wait_send()
    for s in range(4):
        for copy in z_send(s):
            copy.wait_send()

    def drain_x(dz, carry):
        for copy in x_send(dz) + x_forward(dz):
            copy.wait_send()
        return carry

    lax.fori_loop(0, NZ, drain_x, 0)


def layer(tok, ids, gws, wp, eg, eu, ed):
    vmem = pl.BlockSpec(memory_space=pltpu.VMEM)
    hbm = pl.BlockSpec(memory_space=pl.ANY)
    dma = pltpu.SemaphoreType.DMA
    G = GROUPS
    return pl.pallas_call(
        kernel,
        out_shape=jax.ShapeDtypeStruct((TOK, Q), BF16),
        in_specs=[vmem, vmem, vmem, vmem, hbm, hbm, hbm],
        out_specs=vmem,
        scratch_shapes=[
            pltpu.VMEM((G, ROWS, Q), BF16),
            pltpu.VMEM((G + 1, 4, ROWS, Q), BF16),
            pltpu.VMEM((D, H), BF16),
            pltpu.VMEM((D, H), BF16),
            pltpu.VMEM((H, D), BF16),
            pltpu.VMEM((G + 2, 2, 2, ROWS, Q), BF16),
            pltpu.VMEM((G + 2, 2, ROWS, Q), BF16),
            pltpu.VMEM((G + 2, ROWS, Q), BF16),
            pltpu.VMEM((G + 2, ROWS, Q), F32),
            pltpu.VMEM((G + 2, ROWS, Q), BF16),
            pltpu.VMEM((G + 1, ROWS, Q), BF16),
            pltpu.VMEM((G + 1, ROWS, Q), BF16),
            pltpu.VMEM((G, TOK, ROWS), BF16),
            pltpu.VMEM((G, TOK, ROWS), BF16),
            pltpu.VMEM((NX * NY * NZ, TOK), F32),
            pltpu.VMEM((NX * NY * NZ, TOK), F32),
            pltpu.VMEM((NX, NZ, NY, 3, 32, H), BF16),
            dma((G + 1, NZ)), dma((G + 1, NZ)),
            dma((G + 1,)), dma((G + 1,)), dma((G + 1,)), dma((G + 1,)), dma((G + 1,)), dma((G + 1,)),
            dma((G + 2,)), dma((G + 2,)), dma((G + 2,)), dma((G + 2,)),
            dma((G + 1, NZ)), dma((G + 1, NZ)),
            dma, dma,
            dma((4,)), dma((4,)), dma((4,)), dma((4,)),
            dma((NZ,)), dma((NZ,)), dma((NZ,)), dma((NZ,)),
            dma((NZ,)), dma((NZ,)), dma((NZ,)), dma((NZ,)),
            dma((3,)),
        ],
        compiler_params=pltpu.CompilerParams(
            collective_id=0, has_side_effects=True, vmem_limit_bytes=62 * 1024 * 1024
        ),
    )(tok, ids, gws, wp, eg, eu, ed)


def body(tokens, expert_ids, gate_weights, shared_gate, shared_up, shared_down,
         expert_gate, expert_up, expert_down):
    pad = ((0, 2), (0, 0))
    ids = jnp.pad(expert_ids.T, pad)
    gws = jnp.pad(gate_weights.T, pad)
    packed = jnp.stack([shared_gate, shared_up, shared_down.T])
    packed = packed.reshape(3, 32, NY, H).transpose(2, 0, 1, 3)
    return layer(tokens, ids, gws, packed, expert_gate, expert_up, expert_down)


def solution(mesh):
    in_specs = (
        P("wide", None), P("wide", None), P("wide", None),
        P("wide", "narrow"), P("wide", "narrow"), P("narrow", "wide"),
        P("wide", None, "narrow"), P("wide", None, "narrow"), P("wide", "narrow", None),
    )
    return jax.shard_map(
        body, mesh=mesh, in_specs=in_specs, out_specs=P("wide", "narrow"), check_vma=False
    )
```

time: 335 us -> 129 us (0.39)
  blocking collectives: 128 us -> 0 us
  Pallas kernels: 0 us -> 116 us
  waiting for transfers between devices: 97.5 us -> 0 us
  matrix products: 29.3 us -> 0 us
  starting transfers between devices: 28.1 us -> 0 us
  other arithmetic: 18.9 us -> 0.7 us
  between operations: 13.6 us -> 0.06 us
  local copies, waits for them, and re-layouts: 19.1 us -> 11.2 us
    all_to_all x2 -> x0, blocking collectives: 128 us -> none  [the longest x1 68.2 us: items_in_groups(): lax.all_to_all(group, axis, split_axis=split_dim, concat_axis=concat_dim,...]
    pallas_call x0 -> x1, Pallas kernels: none -> 116 us  [layer(): pl.pallas_call(kernel, out_shape=jax.ShapeDtypeStruct((TOK, Q), BF16), in...]
    all_gather x2 -> x0, waiting for transfers between devices: 50 us -> none  [the longest x1 50 us: body(): lax.all_gather(shared_down, 'wide', axis=1, tiled=True)]
    all_to_all x3 -> x0, waiting for transfers between devices: 46.9 us -> none  [the longest x1 46.5 us: items_in_groups(): lax.all_to_all(group, axis, split_axis=split_dim, concat_axis=concat_dim,...]
    dot_general x6 -> x0, matrix products: 29.3 us -> none  [the longest x2 11.5 us: expert_ffn(): jnp.dot(hidden, w_down, preferred_element_type=jnp.float32)]
    all_to_all x3 -> x0, starting transfers between devices: 28 us -> none  [the longest x1 10.2 us: items_in_groups(): lax.all_to_all(group, axis, split_axis=split_dim, concat_axis=concat_dim,...]
    gather x2 -> x0, local copies, waits for them, and re-layouts: 9.38 us -> none  [the longest x1 6.06 us: body(): tokens[token_of]]
    reduce_sum x4 -> x0, other arithmetic: 7.95 us -> none  [the longest x2 5.57 us: sum_at_owner(): return jnp.sum(blocks.astype(jnp.float32), axis=0)]
  transfers between devices with their start and end apart: 5 -> 0, of which waited for: 3 -> 0; matrix products, arithmetic and copies ran while one was open for 19% -> 0% of each run, Pallas kernels for 0% -> 0%
where the time goes in v1:
time: 129 us; the launch traced here: 128 us
  Pallas kernels  116 us (90%)
  local copies, waits for them, and re-layouts  11.2 us (9%)
    pallas_call x1, Pallas kernels, layer(): pl.pallas_call(kernel, out_shape=jax.ShapeDtypeStruct((TOK, Q), BF16), in...  116 us
    unnamed x5, local copies, waits for them, and re-layouts  5.83 us
    another operation x6, local copies, waits for them, and re-layouts, body(): packed = jnp.stack([shared_gate, shared_up, shared_down.T])  2.77 us

profile of v1, /device:TPU:1, one launch (start us, length us, event | category | flops | bytes accessed | tf_op | source)
XLA Modules:
  0.0 128.4 jit_solution(8632637695168681597)
XLA Ops:
  0.0 1.3 pad.8.ids
  1.3 1.3 pad.9.gws
  2.6 0.9 stack.12
  3.5 0.9 stack.13
  4.4 0.9 stack.14
  5.4 0.7 maximum_bitcast_fusion.wp
  6.1 0.0 copy-start
  6.1 2.7 %copy.15.eg = bf16[1,2048,352]{2,1,0:T(8,128)(2,1)} copy(bf16[1,2048,352]{1,2,0:T(8,128)(2,1)} %param.15) | data formatting | bytes 2883584 | tf_op args[6]
  8.8 0.0 copy-done
  8.8 1.6 %copy.16.eu = bf16[1,2048,352]{2,1,0:T(8,128)(2,1)} copy(bf16[1,2048,352]{1,2,0:T(8,128)(2,1)S(1)} %copy-done) | data formatting | bytes 2883584 | tf_op args[7]
  10.3 116.5 %shard_map.91 = bf16[128,512]{1,0:T(8,128)(2,1)} custom-call(bf16[128,2048]{1,0:T(8,128)(2,1)} %tok.1, s32[8,128]{1,0:T(8,128)} %pad.8.ids, f32[8,128]{1,0:T(8,128)} %pad.9.gws, bf16[2,3,32,352]{3,2,1,0:T(8,128)(2,1)} %maximum_bitcast_fusion.wp, bf16[1,2048,352]{2,1,0:T(8,128)(2,1)} %copy.15.eg, bf16[1,2048,352]{2,1,0:T(8,128)(2,1)} %copy.16.eu, ...), custom_call_target="tpu_custom_call" | custom-call | tf_op jit(solution)/shard_map/pallas_call | solution.py:421
  126.8 1.6 %copy.18 = bf16[128,512]{1,0:T(8,128)(2,1)} copy(bf16[128,512]{1,0:T(8,128)(2,1)} %shard_map.91) | data formatting | bytes 262144
  (3 shorter events, 0.0 us)
Async XLA Ops:
  6.1 2.7 %copy-start = (bf16[1,2048,352]{1,2,0:T(8,128)(2,1)S(1)}, bf16[1,2048,352]{1,2,0:T(8,128)(2,1)}, u32[]{:S(2)}) copy-start(bf16[1,2048,352]{1,2,0:T(8,128)(2,1)} %param.16) | copy-start | bytes 4325380

commit v2 on v1

v2 whole, which is shorter than its diff:
```python
import jax
import jax.numpy as jnp
from jax import lax
from jax.experimental import pallas as pl
from jax.experimental.pallas import tpu as pltpu
from jax.sharding import PartitionSpec as P

MESH = pl.DeviceIdType.MESH
BF16 = jnp.bfloat16
F32 = jnp.float32

NX, NY, NZ = 4, 2, 8
CAP = 16
GROUPS = NX * NY
ROWS = NZ * CAP
TOK = 128
D = 2048
Q = D // 4
H = 352
ORDER = (0, 7, 1, 6, 2, 5, 3, 4)
UNITS = (0, 7, 1, 6, 2, 5, 3, 4)
LAG = (2, 3, 4, 5, 6, 8)
TOKEN_RING = (1, 2, 3, 4)
RING = (1, 3, 4, 6, 7)
X_SEND = (1, 3, 4, 5, 6, 7, 8, 8)
FORWARD = (4, 6, 7, 8, 9, 10, 11, 12)
SHARED = 13


def silu_mul(g, u):
    return (g * jax.nn.sigmoid(g) * u).astype(BF16)


def dot(a, b):
    return jnp.dot(a, b, preferred_element_type=F32)


def dot_t(a, b):
    return lax.dot_general(a, b, (((1,), (1,)), ((), ())), preferred_element_type=F32)


def kernel(
    tok, ids, gws, sg, su, sd, eg, eu, ed, out,
    wp, mine, mg, tblk, outg, full, wg, wu, wd, pbuf, r1, sbuf, keep, r2, fin, ret, zout, zin,
    whi, wlo, own, wall,
    mg_s, mg_r, tp_s, th_s, tc_s, tc_r, td_s, td_r,
    ds_s, ds_r, a1_s, a1_r, a2_s, a2_r, b_s, b_r, r1_s, r1_r, r2_s, r2_r, rt_s, rt_r, zr_s, zr_r,
    w0_s, w0_r, zc_s, zc_r, zd_s, zd_r, xp_s, xp_r, xm_s, xm_r, xf_s, xf_r, xg_s, xg_r, l_s,
):
    w = lax.axis_index("wide")
    n = lax.axis_index("narrow")
    x, yh, z = w // (NY * NZ), (w // NZ) % NY, w % NZ
    a, c = n // 2, n % 2

    def dev(xx, yy, zz):
        return ((xx % NX) * NY + yy % NY) * NZ + zz % NZ

    mate = (w, 2 * a + 1 - c)
    over = (w, 2 * (1 - a) + c)
    n_mate, n_over, n_diag = mate[1], over[1], 2 * (1 - a) + 1 - c
    partner = (dev(x, yh + 1, z), n)

    def peer(dx, dy, back=False):
        if back:
            dx, dy = NX - dx, NY - dy
        return (dev(x + dx, yh + dy, z), n if dy % NY == 0 else n_over)

    def remote(src, dst, ssem, rsem, device):
        return pltpu.make_async_remote_copy(
            src_ref=src, dst_ref=dst, send_sem=ssem, recv_sem=rsem,
            device_id=device, device_id_type=MESH,
        )

    def wait(ref, sem):
        pltpu.make_async_copy(ref, ref, sem).wait()

    barrier = pltpu.get_barrier_semaphore()
    friends = [peer(j % NX, j // NX) for j in range(1, GROUPS)]
    friends += [(dev(x, yh, z + dz), n) for dz in range(1, NZ)]
    friends += [mate, over, partner]
    for friend in friends:
        pl.semaphore_signal(barrier, inc=1, device_id=friend, device_id_type=MESH)

    loads = (
        pltpu.make_async_copy(eg.at[0], wg, l_s.at[0]),
        pltpu.make_async_copy(eu.at[0], wu, l_s.at[1]),
        pltpu.make_async_copy(ed.at[0], wd, l_s.at[2]),
    )
    for load in loads:
        load.start()

    for k, shard in enumerate((sg, su, sd)):
        for half in range(NY):
            wp[half, k] = shard[:, half * H : (half + 1) * H]
    wall[x, z, yh] = wp[yh]
    quarter = pl.ds(pl.multiple_of(n * Q, Q), Q)
    tblk[z] = tok[:, quarter]
    mine[:6] = ids[...].astype(F32)
    mine[8:14] = gws[...]
    mg[z] = mine[...]
    upper = jnp.where(
        lax.broadcasted_iota(jnp.int32, (TOK, TOK), 0)
        < lax.broadcasted_iota(jnp.int32, (TOK, TOK), 1),
        1.0, 0.0,
    ).astype(BF16)
    row = lax.broadcasted_iota(jnp.int32, (ROWS, GROUPS), 0) // CAP
    spread = jnp.where(
        (((x + row % NX) % NX) * NY + (yh + row // NX) % NY)
        == lax.broadcasted_iota(jnp.int32, (ROWS, GROUPS), 1),
        1.0, 0.0,
    ).astype(BF16)
    slot = (lax.broadcasted_iota(jnp.int32, (ROWS, TOK), 0) % CAP).astype(F32)
    expert = (lax.broadcasted_iota(jnp.int32, (GROUPS, TOK), 0) * NZ + z).astype(F32)

    pl.semaphore_wait(barrier, len(friends))

    w0 = remote(wp.at[1 - yh], wall.at[x, z, yh], w0_s, w0_r, partner)
    w0.start()

    def meta_send(dz):
        return remote(mine, mg.at[z], mg_s, mg_r.at[dz], (dev(x, yh, z + dz), n))

    def block(dz):
        return tblk.at[(z + dz) % NZ]

    def token_send(s):
        up, down = block(NZ - s), block(s)
        up_src, down_src = up, down
        if s == 0:
            up_src = down_src = tok.at[:, quarter]
        if s == 3:
            up_src = up = up.at[: TOK // 2]
            down_src = down = down.at[TOK // 2 :]
        return (
            remote(up_src, up, tc_s.at[s], tc_r.at[s], (dev(x, yh, z + 1), n)),
            remote(down_src, down, td_s.at[s], td_r.at[s], (dev(x, yh, z + NZ - 1), n)),
        )

    def token_ring(s):
        if s < 4:
            wait(block(NZ - s), tc_r.at[s - 1])
            wait(block(s), td_r.at[s - 1])
            for copy in token_send(s):
                copy.start()
        else:
            wait(block(4).at[: TOK // 2], tc_r.at[3])
            wait(block(4).at[TOK // 2 :], td_r.at[3])

    for copy in token_send(0):
        copy.start()
    for dz in range(1, NZ):
        meta_send(dz).start()
    to_partner = remote(
        tok.at[:, quarter], full.at[GROUPS, n_over],
        tp_s, ds_r.at[GROUPS], (partner[0], n_over),
    )

    def offset(k):
        early = (k + 1) // 2 * (1 - k % 2 * 2)
        late = 4 - (k - 4) // 2 + k % 2 * (1 - (k - 4) // 2 * 2)
        return (early * ((7 - k) // 4) + late * (k // 4) + NZ) % NZ

    def part_of(j):
        return pl.ds(j * CAP, CAP)

    def row_send(k, j):
        return remote(
            outg.at[k, part_of(j)], full.at[k, peer(j % NX, j // NX)[1], part_of(j)],
            ds_s, ds_r.at[k], peer(j % NX, j // NX),
        )

    def select(k):
        zb = (z + offset(k)) % NZ

        @pl.when(k > 0)
        def _():
            dz = (NZ - offset(k)) % NZ
            wait(mg.at[zb], mg_r.at[dz])

        named = jnp.zeros((GROUPS, TOK), F32)
        weight = jnp.zeros((GROUPS, TOK), F32)
        for t in range(6):
            hit = mg[zb, t : t + 1, :] == expert
            named = jnp.where(hit, 1.0, named)
            weight = jnp.where(hit, mg[zb, 8 + t : 9 + t, :], weight)
        before = dot(named.astype(BF16), upper)
        rank = jnp.where(named > 0.0, before, -1.0)
        hit = dot(spread, rank.astype(BF16)) == slot
        outg[k] = dot(jnp.where(hit, 1.0, 0.0).astype(BF16), tblk[zb]).astype(BF16)
        for j in range(1, GROUPS):
            row_send(k, j).start()
        full[k, n, :CAP] = outg[k, :CAP]
        w_hi = weight.astype(BF16)
        w_lo = (weight - w_hi.astype(F32)).astype(BF16)
        zero = jnp.zeros((ROWS, TOK), F32)
        whi[k] = jnp.where(hit, dot(spread, w_hi), zero).T.astype(BF16)
        wlo[k] = jnp.where(hit, dot(spread, w_lo), zero).T.astype(BF16)

    def unit(xx, dz):
        return wall.at[xx % NX, (z + dz) % NZ]

    def x_send(dz):
        u = unit(x, dz)
        return (
            remote(u, u, xp_s, xp_r.at[dz], (dev(x + 1, yh, z), n)),
            remote(u, u, xm_s, xm_r.at[dz], (dev(x + NX - 1, yh, z), n)),
        )

    def x_forward(dz):
        lower = unit(x + NX - 1, dz).at[0]
        upper = unit(x + 1, dz).at[1]
        return (
            remote(lower, lower, xf_s, xf_r, (dev(x + 1, yh, z), n)),
            remote(upper, upper, xg_s, xg_r, (dev(x + NX - 1, yh, z), n)),
        )

    def z_send(s):
        up, down = unit(x, NZ - s), unit(x, s)
        if s == 3:
            up, down = up.at[0], down.at[1]
        return (
            remote(up, up, zc_s.at[s], zc_r.at[s], (dev(x, yh, z + 1), n)),
            remote(down, down, zd_s.at[s], zd_r.at[s], (dev(x, yh, z + NZ - 1), n)),
        )

    def ring(s):
        if s == 0:
            wait(wall.at[x, z, 1 - yh], w0_r)
        elif s < 4:
            wait(unit(x, NZ - s), zc_r.at[s - 1])
            wait(unit(x, s), zd_r.at[s - 1])
        else:
            wait(unit(x, 4).at[0], zc_r.at[3])
            wait(unit(x, 4).at[1], zd_r.at[3])
        if s < 4:
            for copy in z_send(s):
                copy.start()

    def forward(dz):
        wait(unit(x + NX - 1, dz), xp_r.at[dz])
        wait(unit(x + 1, dz), xm_r.at[dz])
        for copy in x_forward(dz):
            copy.start()

    to_partner.start()
    for load in loads:
        load.wait()

    def gather_mate(i):
        return remote(full.at[i, n], full.at[i, n], a1_s, a1_r.at[i], mate)

    def gather_over(i):
        return remote(full.at[i, n], full.at[i, n], a2_s, a2_r.at[i], over)

    def gather_diag(i):
        return remote(full.at[i, n_over], full.at[i, n_over], b_s, b_r.at[i], mate)

    def scatter_mate(i):
        return remote(pbuf.at[i, 1 - c], r1.at[i], r1_s, r1_r.at[i], mate)

    def scatter_over(i):
        return remote(sbuf.at[i], r2.at[i], r2_s, r2_r.at[i], over)

    def return_copy(k, j):
        return remote(
            fin.at[k, part_of(j)], ret.at[k, part_of(j)],
            rt_s, rt_r.at[k], peer(j % NX, j // NX, back=True),
        )

    to_home = remote(
        fin.at[GROUPS], ret.at[GROUPS], th_s, rt_r.at[GROUPS],
        (partner[0], n_over),
    )

    def arrive(i):
        @pl.when(i < GROUPS)
        def _():
            wait(full.at[i, n, pl.ds(CAP, ROWS - CAP)], ds_r.at[i])

        @pl.when(i == GROUPS)
        def _():
            wait(full.at[GROUPS, n], ds_r.at[GROUPS])

        gather_over(i).start()
        gather_mate(i).start()

    def pass_on(i):
        wait(full.at[i, n_over], a2_r.at[i])
        gather_diag(i).start()

    def gathered(i):
        wait(full.at[i, n_mate], a1_r.at[i])
        wait(full.at[i, n_diag], b_r.at[i])

    half = ROWS // 2

    def ffn(i):
        gathered(i)
        gp = jnp.zeros((ROWS, H), F32)
        up = jnp.zeros((ROWS, H), F32)
        for q in range(4):
            rows = jnp.concatenate([full[i, q, :half], full[i, (q + 2) % 4, half:]], axis=0)
            gp += dot_t(rows, wg[:, q * Q : (q + 1) * Q])
            up += dot_t(rows, wu[:, q * Q : (q + 1) * Q])
        hidden = silu_mul(gp, up)
        for q in range(4):
            part = dot(hidden, wd[:, q * Q : (q + 1) * Q]).astype(BF16)
            pbuf[i, q % 2, q // 2, :half] = part[:half]
            pbuf[i, q % 2, 1 - q // 2, half:] = part[half:]
        scatter_mate(i).start()

    def add_mate(i):
        wait(r1.at[i], r1_r.at[i])
        sbuf[i] = (pbuf[i, c, 1 - a].astype(F32) + r1[i, 1 - a].astype(F32)).astype(BF16)
        scatter_over(i).start()
        keep[i] = pbuf[i, c, a].astype(F32) + r1[i, a].astype(F32)

    def add_over(i):
        wait(r2.at[i], r2_r.at[i])
        return keep[i] + r2[i].astype(F32)

    def send_home(i):
        fin[i] = add_over(i).astype(BF16)
        for j in range(1, GROUPS):
            return_copy(i, j).start()
        ret[i, :CAP] = fin[i, :CAP]

    def z_return(k):
        return remote(
            zout.at[k], zin.at[k], zr_s, zr_r.at[k], (dev(x, yh, z + offset(k)), n)
        )

    def combine(k):
        wait(ret.at[k, pl.ds(CAP, ROWS - CAP)], rt_r.at[k])
        part = dot(whi[k], ret[k]) + dot(wlo[k], ret[k])

        @pl.when(k == 0)
        def _():
            own[...] = part

        @pl.when(k > 0)
        def _():
            zout[k] = part.astype(BF16)
            z_return(k).start()

    def shared():
        wait(wall.at[0, : NZ // 2], xf_r)
        wait(wall.at[0, : NZ // 2], xg_r)
        gathered(GROUPS)
        gp = jnp.zeros((2 * TOK, H), F32)
        up = jnp.zeros((2 * TOK, H), F32)
        wide_block = NZ * 32
        for k in range(NX * NY):
            xx, yy = k // NY, k % NY
            rows = jnp.concatenate(
                [
                    full[GROUPS, (xx + 2) % 4, :, yy * wide_block : (yy + 1) * wide_block],
                    tok[:, k * wide_block : (k + 1) * wide_block],
                ],
                axis=0,
            )
            gp += dot(rows, wall[xx, :, yy, 0].reshape(wide_block, H))
            up += dot(rows, wall[xx, :, yy, 1].reshape(wide_block, H))
        hidden = silu_mul(gp, up)
        for k in range(NX * NY):
            xx, yy = k // NY, k % NY
            part = dot_t(hidden, wall[xx, :, yy, 2].reshape(wide_block, H)).astype(BF16)
            cols = slice(yy * wide_block, (yy + 1) * wide_block)
            pbuf[GROUPS, xx % 2, 1 - xx // 2, :, cols] = part[:TOK]
            pbuf[GROUPS + 1, xx % 2, xx // 2, :, cols] = part[TOK:]
        scatter_mate(GROUPS).start()
        scatter_mate(GROUPS + 1).start()

    side = {}
    for k, it in enumerate(RING):
        side.setdefault(it, []).append(lambda k=k: ring(k))
    for k in range(NZ):
        side.setdefault(X_SEND[k], []).append(lambda k=k: [c.start() for c in x_send(UNITS[k])])
        side.setdefault(FORWARD[k], []).append(lambda k=k: forward(UNITS[k]))
    side.setdefault(SHARED, []).append(shared)
    side.setdefault(SHARED + 1, []).extend([lambda: add_mate(GROUPS), lambda: add_mate(GROUPS + 1)])

    def step(i, carry):
        for k, it in enumerate(TOKEN_RING):
            @pl.when(i == it)
            def _():
                token_ring(k + 1)

        stages = (
            (0, GROUPS, select), (LAG[0], GROUPS + 1, arrive), (LAG[1], GROUPS + 1, pass_on),
            (LAG[2], GROUPS, ffn), (LAG[3], GROUPS, add_mate), (LAG[4], GROUPS, send_home),
            (LAG[5], GROUPS, combine),
        )
        for lag, count, stage in stages:
            @pl.when((i >= lag) & (i < count + lag))
            def _():
                stage(i - lag)

        for it, jobs in side.items():
            @pl.when(i == it)
            def _():
                for job in jobs:
                    job()

        return carry

    lax.fori_loop(0, GROUPS + LAG[5], step, 0)

    fin[GROUPS] = add_over(GROUPS).astype(BF16)
    to_home.start()
    acc = own[...]
    for k in range(1, GROUPS):
        wait(zin.at[k], zr_r.at[k])
        acc += zin[k].astype(F32)
    acc = acc + add_over(GROUPS + 1)
    wait(ret.at[GROUPS], rt_r.at[GROUPS])
    out[...] = (acc + ret[GROUPS].astype(F32)).astype(BF16)

    w0.wait_send()
    to_partner.wait_send()
    to_home.wait_send()
    wait(outg.at[: GROUPS - 1], ds_s)
    wait(outg.at[: GROUPS - 1], rt_s)
    wait(outg.at[: GROUPS - 1], zr_s)
    wait(mg.at[: NZ - 1], mg_s)
    for sem in (a1_s, a2_s, b_s):
        wait(full.at[:, 0], sem)
    wait(r1, r1_s)
    wait(r2, r2_s)
    wait(wall.at[0], xp_s)
    wait(wall.at[0], xm_s)
    wait(wall.at[0, : NZ // 2], xf_s)
    wait(wall.at[0, : NZ // 2], xg_s)
    for s in range(4):
        for copy in token_send(s) + z_send(s):
            copy.wait_send()


def layer(tok, ids, gws, sg, su, sd, eg, eu, ed):
    vmem = pl.BlockSpec(memory_space=pltpu.VMEM)
    hbm = pl.BlockSpec(memory_space=pl.ANY)
    dma = pltpu.SemaphoreType.DMA
    G = GROUPS
    return pl.pallas_call(
        kernel,
        out_shape=jax.ShapeDtypeStruct((TOK, Q), BF16),
        in_specs=[vmem] * 6 + [hbm] * 3,
        out_specs=vmem,
        scratch_shapes=[
            pltpu.VMEM((NY, 3, 32, H), BF16),
            pltpu.VMEM((16, TOK), F32),
            pltpu.VMEM((NZ, 16, TOK), F32),
            pltpu.VMEM((NZ, TOK, Q), BF16),
            pltpu.VMEM((G, ROWS, Q), BF16),
            pltpu.VMEM((G + 1, 4, ROWS, Q), BF16),
            pltpu.VMEM((H, D), BF16),
            pltpu.VMEM((H, D), BF16),
            pltpu.VMEM((H, D), BF16),
            pltpu.VMEM((G + 2, 2, 2, ROWS, Q), BF16),
            pltpu.VMEM((G + 2, 2, ROWS, Q), BF16),
            pltpu.VMEM((G + 2, ROWS, Q), BF16),
            pltpu.VMEM((G + 2, ROWS, Q), F32),
            pltpu.VMEM((G + 2, ROWS, Q), BF16),
            pltpu.VMEM((G + 1, ROWS, Q), BF16),
            pltpu.VMEM((G + 1, ROWS, Q), BF16),
            pltpu.VMEM((G, TOK, Q), BF16),
            pltpu.VMEM((G, TOK, Q), BF16),
            pltpu.VMEM((G, TOK, ROWS), BF16),
            pltpu.VMEM((G, TOK, ROWS), BF16),
            pltpu.VMEM((TOK, Q), F32),
            pltpu.VMEM((NX, NZ, NY, 3, 32, H), BF16),
            dma, dma((NZ,)), dma, dma,
            dma((4,)), dma((4,)), dma((4,)), dma((4,)),
            dma, dma((G + 1,)), dma, dma((G + 1,)), dma, dma((G + 1,)), dma, dma((G + 1,)),
            dma, dma((G + 2,)), dma, dma((G + 2,)), dma, dma((G + 1,)), dma, dma((G,)),
            dma, dma, dma((4,)), dma((4,)), dma((4,)), dma((4,)),
            dma, dma((NZ,)), dma, dma((NZ,)), dma, dma, dma, dma,
            dma((3,)),
        ],
        compiler_params=pltpu.CompilerParams(
            collective_id=0, has_side_effects=True, vmem_limit_bytes=62 * 1024 * 1024
        ),
    )(tok, ids, gws, sg, su, sd, eg, eu, ed)


def body(tokens, expert_ids, gate_weights, shared_gate, shared_up, shared_down,
         expert_gate, expert_up, expert_down):
    return layer(
        tokens, expert_ids.T, gate_weights.T, shared_gate, shared_up, shared_down.T,
        jnp.swapaxes(expert_gate, 1, 2), jnp.swapaxes(expert_up, 1, 2), expert_down,
    )


def solution(mesh):
    in_specs = (
        P("wide", None), P("wide", None), P("wide", None),
        P("wide", "narrow"), P("wide", "narrow"), P("narrow", "wide"),
        P("wide", None, "narrow"), P("wide", None, "narrow"), P("wide", "narrow", None),
    )
    return jax.shard_map(
        body, mesh=mesh, in_specs=in_specs, out_specs=P("wide", "narrow"), check_vma=False
    )
```

time: 129 us -> 100 us (0.78)
  Pallas kernels: 116 us -> 98.4 us
  local copies, waits for them, and re-layouts: 11.2 us -> 1.57 us
    pallas_call x1, Pallas kernels: 116 us -> 98.4 us  [layer(): pl.pallas_call(kernel, out_shape=jax.ShapeDtypeStruct((TOK, Q), BF16), in...]
    unnamed x5 -> x1, local copies, waits for them, and re-layouts: 5.83 us -> 1.57 us
    another operation x6 -> x0, local copies, waits for them, and re-layouts: 2.77 us -> none  [body(): packed = jnp.stack([shared_gate, shared_up, shared_down.T])]
    pad x2 -> x0, local copies, waits for them, and re-layouts: 2.56 us -> none  [the longest x1 1.28 us: body(): ids = jnp.pad(expert_ids.T, pad)]
where the time goes in v2:
time: 100 us
  Pallas kernels  98.4 us (98%)
  local copies, waits for them, and re-layouts  1.57 us (2%)
    pallas_call x1, Pallas kernels, layer(): pl.pallas_call(kernel, out_shape=jax.ShapeDtypeStruct((TOK, Q), BF16), in...  98.4 us

profile of v2, /device:TPU:1, one launch (start us, length us, event | category | flops | bytes accessed | tf_op | source)
XLA Modules:
  0.0 100.0 jit_solution(6370420878030221953)
XLA Ops:
  0.0 98.4 %shard_map.91 = bf16[128,512]{1,0:T(8,128)(2,1)} custom-call(bf16[128,2048]{1,0:T(8,128)(2,1)} %tok.1, s32[6,128]{1,0:T(8,128)} %bitcast.8, f32[6,128]{1,0:T(8,128)} %bitcast.9, bf16[32,704]{1,0:T(8,128)(2,1)} %sg.1, bf16[32,704]{1,0:T(8,128)(2,1)} %su.1, bf16[32,704]{1,0:T(8,128)(2,1)} %bitcast.7, bf16[1,352,2048]{2,1,0:T(8,128)(2,1)} %bitcast.5, ...), custom_call_target="tpu_custom_call" | custom-call | tf_op jit(solution)/shard_map/pallas_call | solution.py:444
  98.4 1.6 %copy.11 = bf16[128,512]{1,0:T(8,128)(2,1)} copy(bf16[128,512]{1,0:T(8,128)(2,1)} %shard_map.91) | data formatting | bytes 262144

commit v3 on v2

--- a/solution.py
+++ b/solution.py
@@ -19,12 +19,18 @@
 H = 352
 ORDER = (0, 7, 1, 6, 2, 5, 3, 4)
 UNITS = (0, 7, 1, 6, 2, 5, 3, 4)
-LAG = (2, 3, 4, 5, 6, 8)
-TOKEN_RING = (1, 2, 3, 4)
-RING = (1, 3, 4, 6, 7)
-X_SEND = (1, 3, 4, 5, 6, 7, 8, 8)
-FORWARD = (4, 6, 7, 8, 9, 10, 11, 12)
-SHARED = 13
+ORDER = (0, 7, 6, 4, 3, 5, 2, 1)
+TOKEN_RING = (2, 4, 5, 6)
+SELECT = (0, 2, 4, 6, 5, 5, 4, 2)
+ARRIVE = (1, 4, 5, 7, 6, 6, 5, 4, 7)
+PASS_ON = (5, 6, 8, 7, 7, 6, 5)
+FIRST = (3, 4, 5, 7)
+LAG = (5, 6, 7, 8)
+RING = (2, 4, 5, 6, 8)
+X_SEND = (2, 4, 5, 6, 7, 8, 9, 10)
+FORWARD = (5, 7, 8, 9, 10, 11, 12, 13)
+SHARED = 14
+PARTNER = 4
 
 
 def silu_mul(g, u):
@@ -41,9 +47,9 @@
 
 def kernel(
     tok, ids, gws, sg, su, sd, eg, eu, ed, out,
-    wp, mine, mg, tblk, outg, full, wg, wu, wd, pbuf, r1, sbuf, keep, r2, fin, ret, zout, zin,
+    wp, mine, mg, tblk, outw, outg, full, wg, wu, wd, pbuf, r1, sbuf, keep, r2, fin, ret, zout, zin,
     whi, wlo, own, wall,
-    mg_s, mg_r, tp_s, th_s, tc_s, tc_r, td_s, td_r,
+    mg_s, mg_r, tp_s, th_s, dw_s, dw_r, dp_s, dp_r, tc_s, tc_r, td_s, td_r,
     ds_s, ds_r, a1_s, a1_r, a2_s, a2_r, b_s, b_r, r1_s, r1_r, r2_s, r2_r, rt_s, rt_r, zr_s, zr_r,
     w0_s, w0_r, zc_s, zc_r, zd_s, zd_r, xp_s, xp_r, xm_s, xm_r, xf_s, xf_r, xg_s, xg_r, l_s,
 ):
@@ -150,15 +156,18 @@
         copy.start()
     for dz in range(1, NZ):
         meta_send(dz).start()
-    to_partner = remote(
-        tok.at[:, quarter], full.at[GROUPS, n_over],
-        tp_s, ds_r.at[GROUPS], (partner[0], n_over),
+    other_quarter = pl.ds(pl.multiple_of(n_over * Q, Q), Q)
+    to_partner = (
+        remote(
+            tok.at[:, quarter], full.at[GROUPS, n_over],
+            tp_s, ds_r.at[GROUPS], (partner[0], n_over),
+        ),
+        remote(tok.at[:, other_quarter], full.at[GROUPS, n], dp_s, dp_r, (partner[0], n_over)),
     )
 
     def offset(k):
-        early = (k + 1) // 2 * (1 - k % 2 * 2)
-        late = 4 - (k - 4) // 2 + k % 2 * (1 - (k - 4) // 2 * 2)
-        return (early * ((7 - k) // 4) + late * (k // 4) + NZ) % NZ
+        steps = [(k + GROUPS - j) // GROUPS * (ORDER[j] - ORDER[j - 1]) for j in range(1, GROUPS)]
+        return ORDER[0] + sum(steps)
 
     def part_of(j):
         return pl.ds(j * CAP, CAP)
@@ -169,14 +178,17 @@
             ds_s, ds_r.at[k], peer(j % NX, j // NX),
         )
 
+    def row_send_wide(j):
+        target = peer(j % NX, j // NX)
+        return remote(
+            outw.at[part_of(j)], full.at[0, n_over if j < NX else n, part_of(j)],
+            dw_s, dw_r, target,
+        )
+
     def select(k):
         zb = (z + offset(k)) % NZ
-
-        @pl.when(k > 0)
-        def _():
-            dz = (NZ - offset(k)) % NZ
-            wait(mg.at[zb], mg_r.at[dz])
-
+        if k > 0:
+            wait(mg.at[zb], mg_r.at[(NZ - offset(k)) % NZ])
         named = jnp.zeros((GROUPS, TOK), F32)
         weight = jnp.zeros((GROUPS, TOK), F32)
         for t in range(6):
@@ -186,10 +198,16 @@
         before = dot(named.astype(BF16), upper)
         rank = jnp.where(named > 0.0, before, -1.0)
         hit = dot(spread, rank.astype(BF16)) == slot
-        outg[k] = dot(jnp.where(hit, 1.0, 0.0).astype(BF16), tblk[zb]).astype(BF16)
+        pick = jnp.where(hit, 1.0, 0.0).astype(BF16)
+        outg[k] = dot(pick, tblk[zb]).astype(BF16)
         for j in range(1, GROUPS):
             row_send(k, j).start()
         full[k, n, :CAP] = outg[k, :CAP]
+        if k == 0:
+            outw[...] = dot(pick, tok[:, other_quarter]).astype(BF16)
+            for j in range(1, GROUPS):
+                row_send_wide(j).start()
+            full[0, n_over, :CAP] = outw[:CAP]
         w_hi = weight.astype(BF16)
         w_lo = (weight - w_hi.astype(F32)).astype(BF16)
         zero = jnp.zeros((ROWS, TOK), F32)
@@ -242,7 +260,6 @@
         for copy in x_forward(dz):
             copy.start()
 
-    to_partner.start()
     for load in loads:
         load.wait()
 
@@ -273,15 +290,17 @@
     )
 
     def arrive(i):
-        @pl.when(i < GROUPS)
-        def _():
+        if i < GROUPS:
             wait(full.at[i, n, pl.ds(CAP, ROWS - CAP)], ds_r.at[i])
-
-        @pl.when(i == GROUPS)
-        def _():
+        else:
             wait(full.at[GROUPS, n], ds_r.at[GROUPS])
-
-        gather_over(i).start()
+            wait(full.at[GROUPS, n_over], dp_r)
+        if i == 0:
+            wait(full.at[0, n_over, pl.ds(CAP, ROWS - CAP)], dw_r)
+        if i in (0, GROUPS):
+            gather_diag(i).start()
+        else:
+            gather_over(i).start()
         gather_mate(i).start()
 
     def pass_on(i):
@@ -372,39 +391,44 @@
         scatter_mate(GROUPS + 1).start()
 
     side = {}
-    for k, it in enumerate(RING):
-        side.setdefault(it, []).append(lambda k=k: ring(k))
-    for k in range(NZ):
-        side.setdefault(X_SEND[k], []).append(lambda k=k: [c.start() for c in x_send(UNITS[k])])
-        side.setdefault(FORWARD[k], []).append(lambda k=k: forward(UNITS[k]))
-    side.setdefault(SHARED, []).append(shared)
-    side.setdefault(SHARED + 1, []).extend([lambda: add_mate(GROUPS), lambda: add_mate(GROUPS + 1)])
-
-    def step(i, carry):
-        for k, it in enumerate(TOKEN_RING):
+    for its, job in (
+        (TOKEN_RING, lambda k: token_ring(k + 1)),
+        (SELECT, select),
+        (ARRIVE, arrive),
+        (PASS_ON, lambda k: pass_on(k + 1)),
+    ):
+        for k, it in enumerate(its):
+            side.setdefault(it, []).append((job, k))
+    late = {}
+    for its, job in (
+        (RING, ring),
+        (X_SEND, lambda k: [copy.start() for copy in x_send(UNITS[k])]),
+        (FORWARD, lambda k: forward(UNITS[k])),
+        ((PARTNER,), lambda k: [copy.start() for copy in to_partner]),
+        ((SHARED,), lambda k: shared()),
+        ((SHARED + 1,) * 2, lambda k: add_mate(GROUPS + k)),
+    ):
+        for k, it in enumerate(its):
+            late.setdefault(it, []).append((job, k))
+
+    def run(jobs, i):
+        for it, todo in jobs.items():
             @pl.when(i == it)
             def _():
-                token_ring(k + 1)
-
-        stages = (
-            (0, GROUPS, select), (LAG[0], GROUPS + 1, arrive), (LAG[1], GROUPS + 1, pass_on),
-            (LAG[2], GROUPS, ffn), (LAG[3], GROUPS, add_mate), (LAG[4], GROUPS, send_home),
-            (LAG[5], GROUPS, combine),
-        )
-        for lag, count, stage in stages:
-            @pl.when((i >= lag) & (i < count + lag))
+                for job, k in todo:
+                    job(k)
+
+    def step(i, carry):
+        run(side, i)
+        for first, lag, stage in zip(FIRST, LAG, (ffn, add_mate, send_home, combine)):
+            @pl.when((i == first) | ((i > lag) & (i < GROUPS + lag)))
             def _():
-                stage(i - lag)
-
-        for it, jobs in side.items():
-            @pl.when(i == it)
-            def _():
-                for job in jobs:
-                    job()
-
+                stage((i - lag) * ((i + 63 - lag) // 64))
+
+        run(late, i)
         return carry
 
-    lax.fori_loop(0, GROUPS + LAG[5], step, 0)
+    lax.fori_loop(0, GROUPS + LAG[3], step, 0)
 
     fin[GROUPS] = add_over(GROUPS).astype(BF16)
     to_home.start()
@@ -417,14 +441,17 @@
     out[...] = (acc + ret[GROUPS].astype(F32)).astype(BF16)
 
     w0.wait_send()
-    to_partner.wait_send()
+    for copy in to_partner:
+        copy.wait_send()
     to_home.wait_send()
     wait(outg.at[: GROUPS - 1], ds_s)
     wait(outg.at[: GROUPS - 1], rt_s)
     wait(outg.at[: GROUPS - 1], zr_s)
     wait(mg.at[: NZ - 1], mg_s)
-    for sem in (a1_s, a2_s, b_s):
-        wait(full.at[:, 0], sem)
+    wait(full.at[:, 0], a1_s)
+    wait(full.at[: GROUPS - 1, 0], a2_s)
+    wait(full.at[:, 0], b_s)
+    wait(outg.at[0, : ROWS - CAP], dw_s)
     wait(r1, r1_s)
     wait(r2, r2_s)
     wait(wall.at[0], xp_s)
@@ -451,6 +478,7 @@
             pltpu.VMEM((16, TOK), F32),
             pltpu.VMEM((NZ, 16, TOK), F32),
             pltpu.VMEM((NZ, TOK, Q), BF16),
+            pltpu.VMEM((ROWS, Q), BF16),
             pltpu.VMEM((G, ROWS, Q), BF16),
             pltpu.VMEM((G + 1, 4, ROWS, Q), BF16),
             pltpu.VMEM((H, D), BF16),
@@ -469,7 +497,7 @@
             pltpu.VMEM((G, TOK, ROWS), BF16),
             pltpu.VMEM((TOK, Q), F32),
             pltpu.VMEM((NX, NZ, NY, 3, 32, H), BF16),
-            dma, dma((NZ,)), dma, dma,
+            dma, dma((NZ,)), dma, dma, dma, dma, dma, dma,
             dma((4,)), dma((4,)), dma((4,)), dma((4,)),
             dma, dma((G + 1,)), dma, dma((G + 1,)), dma, dma((G + 1,)), dma, dma((G + 1,)),
             dma, dma((G + 2,)), dma, dma((G + 2,)), dma, dma((G + 1,)), dma, dma((G,)),

time: 100 us -> 99 us (0.990)
  Pallas kernels: 98.4 us -> 97.3 us
    pallas_call x1, Pallas kernels: 98.4 us -> 97.3 us  [layer(): pl.pallas_call(kernel, out_shape=jax.ShapeDtypeStruct((TOK, Q), BF16), in...]
where the time goes in v3:
time: 99 us; the launch traced here: 98.8 us
  Pallas kernels  97.3 us (98%)
  local copies, waits for them, and re-layouts  1.57 us (2%)
    pallas_call x1, Pallas kernels, layer(): pl.pallas_call(kernel, out_shape=jax.ShapeDtypeStruct((TOK, Q), BF16), in...  97.3 us

profile of v3, /device:TPU:1, one launch (start us, length us, event | category | flops | bytes accessed | tf_op | source)
XLA Modules:
  0.0 98.8 jit_solution(9053256714597048435)
XLA Ops:
  0.0 97.3 %shard_map.91 = bf16[128,512]{1,0:T(8,128)(2,1)} custom-call(bf16[128,2048]{1,0:T(8,128)(2,1)} %tok.1, s32[6,128]{1,0:T(8,128)} %bitcast.8, f32[6,128]{1,0:T(8,128)} %bitcast.9, bf16[32,704]{1,0:T(8,128)(2,1)} %sg.1, bf16[32,704]{1,0:T(8,128)(2,1)} %su.1, bf16[32,704]{1,0:T(8,128)(2,1)} %bitcast.7, bf16[1,352,2048]{2,1,0:T(8,128)(2,1)} %bitcast.5, ...), custom_call_target="tpu_custom_call" | custom-call | tf_op jit(solution)/shard_map/pallas_call | solution.py:471
  97.3 1.6 %copy.11 = bf16[128,512]{1,0:T(8,128)(2,1)} copy(bf16[128,512]{1,0:T(8,128)(2,1)} %shard_map.91) | data formatting | bytes 262144

commit v4 on v3

--- a/solution.py
+++ b/solution.py
@@ -396,6 +396,8 @@
         (SELECT, select),
         (ARRIVE, arrive),
         (PASS_ON, lambda k: pass_on(k + 1)),
+        ((SHARED,), lambda k: shared()),
+        ((SHARED + 1,) * 2, lambda k: add_mate(GROUPS + k)),
     ):
         for k, it in enumerate(its):
             side.setdefault(it, []).append((job, k))
@@ -405,8 +407,6 @@
         (X_SEND, lambda k: [copy.start() for copy in x_send(UNITS[k])]),
         (FORWARD, lambda k: forward(UNITS[k])),
         ((PARTNER,), lambda k: [copy.start() for copy in to_partner]),
-        ((SHARED,), lambda k: shared()),
-        ((SHARED + 1,) * 2, lambda k: add_mate(GROUPS + k)),
     ):
         for k, it in enumerate(its):
             late.setdefault(it, []).append((job, k))

time: 99 us -> 99.2 us (level)
  no operation moved by 1% of the time
where the time goes in v4:
time: 99.2 us; the launch traced here: 99.1 us
  Pallas kernels  97.6 us (98%)
  local copies, waits for them, and re-layouts  1.57 us (2%)
    pallas_call x1, Pallas kernels, layer(): pl.pallas_call(kernel, out_shape=jax.ShapeDtypeStruct((TOK, Q), BF16), in...  97.6 us

profile of v4, /device:TPU:1, one launch (start us, length us, event | category | flops | bytes accessed | tf_op | source)
XLA Modules:
  0.0 99.1 jit_solution(10146341140688479403)
XLA Ops:
  0.0 97.6 %shard_map.91 = bf16[128,512]{1,0:T(8,128)(2,1)} custom-call(bf16[128,2048]{1,0:T(8,128)(2,1)} %tok.1, s32[6,128]{1,0:T(8,128)} %bitcast.8, f32[6,128]{1,0:T(8,128)} %bitcast.9, bf16[32,704]{1,0:T(8,128)(2,1)} %sg.1, bf16[32,704]{1,0:T(8,128)(2,1)} %su.1, bf16[32,704]{1,0:T(8,128)(2,1)} %bitcast.7, bf16[1,352,2048]{2,1,0:T(8,128)(2,1)} %bitcast.5, ...), custom_call_target="tpu_custom_call" | custom-call | tf_op jit(solution)/shard_map/pallas_call | solution.py:471
  97.6 1.6 %copy.11 = bf16[128,512]{1,0:T(8,128)(2,1)} copy(bf16[128,512]{1,0:T(8,128)(2,1)} %shard_map.91) | data formatting | bytes 262144
